TPU v7x, 32 devices: a whole 2x2x4 slice. The times are simulated.
32 devices in a mesh: row: 4 (over y, x), col: 8 (over z, core).
Axes of the slice: x: 2, y: 2, z: 4, core: 2. Of those that a mesh axis runs over, the one named last changes fastest.
Arguments:
- initial_field: float32 [256, 256, 256], P(('row', 'col')), may hold values from -5 to 5
Outputs:
- advanced_field: float32 [256, 256, 256], P(('row', 'col'))
All inputs are finite; a program needn't handle non-finite values.
Results may differ from a plain program's by a relative error of at most 0.0003.
Values sent between devices are 32-bit elements; how exact they have to be, the bound alone decides.
A program may use at most 128 MiB of HBM per device.

v0:
```python
import math

import jax
import jax.numpy as jnp
from jax import lax
from jax.sharding import PartitionSpec as P

growth_rate = 0.3
quadratic = 1.0
time_step = 0.2
wave_scale = 4.0


def wavenumbers(count, offset, length):
    indices = offset + jnp.arange(count)
    signed = jnp.where(indices * 2 < length, indices, indices - length)
    return wave_scale * signed.astype(jnp.float32) / length


def phi_values(argument):
    within = jnp.abs(argument) < 1.0
    inside = jnp.where(within, argument, 0.0)
    outside = jnp.where(within, 2.0, argument)
    series = []
    for degree in (1, 2, 3):
        running = jnp.zeros_like(argument) + 1.0 / math.factorial(11 + degree)
        for exponent in range(10, -1, -1):
            running = running * inside + 1.0 / math.factorial(exponent + degree)
        series.append(running)
    growth_term = jnp.exp(outside)
    closed_one = (growth_term - 1.0) / outside
    closed_two = (growth_term - 1.0 - outside) / (outside * outside)
    closed_three = (growth_term - 1.0 - outside - 0.5 * outside * outside) / (
        outside * outside * outside
    )
    return (
        jnp.where(within, series[0], closed_one),
        jnp.where(within, series[1], closed_two),
        jnp.where(within, series[2], closed_three),
    )


def step_factors(ksq):
    lin = growth_rate - (1.0 - ksq) * (1.0 - ksq)
    scaled = time_step * lin
    half_phi, _, _ = phi_values(0.5 * scaled)
    first_phi, second_phi, third_phi = phi_values(scaled)
    e_half = jnp.exp(0.5 * scaled)
    q_half = 0.5 * time_step * half_phi
    e_full = jnp.exp(scaled)
    f_one = time_step * (first_phi - 3.0 * second_phi + 4.0 * third_phi)
    f_two = time_step * (second_phi - 2.0 * third_phi)
    f_three = time_step * (4.0 * third_phi - second_phi)
    return (e_half, q_half, e_full, f_one, f_two, f_three)


def reaction(values):
    return quadratic * values * values - values * values * values


def dft_tables(length):
    modes = jnp.arange(length, dtype=jnp.int32)
    product = jnp.mod(modes[:, None] * modes[None, :], length)
    angle = 2.0 * math.pi / length * product.astype(jnp.float32)
    cosine = jnp.cos(angle)
    sine = jnp.sin(angle)
    forward = jnp.stack([jnp.stack([cosine, -sine]), jnp.stack([sine, cosine])])
    inverse = jnp.stack([jnp.stack([cosine, sine]), jnp.stack([-sine, cosine])]) / length
    return (forward, inverse)


def contract(form, left, right):
    return jnp.einsum(
        form, left, right, precision=lax.Precision.HIGHEST, preferred_element_type=jnp.float32
    )


def spectra_move(lower, upper):
    return (
        lax.all_to_all(lower, ("row", "col"), split_axis=0, concat_axis=0, tiled=True),
        lax.all_to_all(upper, ("row", "col"), split_axis=0, concat_axis=0, tiled=True),
    )


def fields_move(lower, upper):
    return (
        lax.all_to_all(lower, ("row", "col"), split_axis=0, concat_axis=0, tiled=True),
        lax.all_to_all(upper, ("row", "col"), split_axis=0, concat_axis=0, tiled=True),
    )


def body(initial_field):
    devices_all = lax.axis_size("row") * lax.axis_size("col")
    rows_x, size_y, size_z = initial_field.shape
    size_x = rows_x * devices_all
    share_y = size_y // devices_all
    half_z = size_z // 2
    forward_x, inverse_x = dft_tables(size_x)
    forward_y, inverse_y = dft_tables(size_y)
    forward_z, inverse_z = dft_tables(size_z)
    table_zf = forward_z[0]
    table_zi = inverse_z[:, 0]
    table_yf = forward_y.reshape((2, 2, size_y, devices_all, share_y))
    table_xf = forward_x.reshape((2, 2, devices_all, rows_x, size_x))
    table_xi = inverse_x.reshape((2, 2, size_x, devices_all, rows_x))
    table_yi = inverse_y.reshape((2, 2, devices_all, share_y, size_y))
    modes_z = half_z + 1
    zf_low = table_zf[:, :, :half_z]
    zf_high = table_zf[:, :, half_z : half_z + 1]
    weight = jnp.where(jnp.arange(half_z) == 0, 1.0, 2.0).astype(jnp.float32)
    zi_low = table_zi[:, :half_z] * weight[None, :, None]
    zi_high = table_zi[:, half_z : half_z + 1]
    offset = lax.axis_index(("row", "col")) * share_y
    wave_y = wavenumbers(share_y, offset, size_y)
    wave_z = wavenumbers(modes_z, 0, size_z)
    wave_x = wavenumbers(size_x, 0, size_x)
    ksq = wave_y[:, None, None] ** 2 + wave_z[None, :, None] ** 2 + wave_x[None, None, :] ** 2
    e_half, q_half, e_full, f_one, f_two, f_three = step_factors(ksq)

    def forward_all(values):
        low_z = contract("fxyn,qnk->fqxyk", values, zf_low)
        high_z = contract("fxyn,qnk->fqxyk", values, zf_high)
        low_y = contract("fpxnz,pqnsl->sfqxlz", low_z, table_yf)
        high_y = contract("fpxnz,pqnsl->sfqxlz", high_z, table_yf)
        low_got, high_got = spectra_move(low_y, high_y)
        low_x = contract("sfpmlz,pqsmk->fqlzk", low_got, table_xf)
        high_x = contract("sfpmlz,pqsmk->fqlzk", high_got, table_xf)
        return jnp.concatenate([low_x, high_x], axis=3)

    def inverse_all(spectra):
        low_s = spectra[:, :, :, :half_z]
        high_s = spectra[:, :, :, half_z:]
        low_x = contract("fplzk,pqksm->sfqmlz", low_s, table_xi)
        high_x = contract("fplzk,pqksm->sfqmlz", high_s, table_xi)
        low_got, high_got = fields_move(low_x, high_x)
        low_y = contract("sfpmlz,pqsln->fqmnz", low_got, table_yi)
        high_y = contract("sfpmlz,pqsln->fqmnz", high_got, table_yi)
        return contract("fpmnk,pkz->fmnz", low_y, zi_low) + contract(
            "fpmnk,pkz->fmnz", high_y, zi_high
        )

    def react_spectrum(spectrum):
        physical = inverse_all(spectrum[None])
        return forward_all(reaction(physical))[0]

    stacked = jnp.stack([initial_field, reaction(initial_field)])
    spectra = forward_all(stacked)
    state_hat = spectra[0]
    react_u = spectra[1]
    first_hat = e_half * state_hat + q_half * react_u
    react_a = react_spectrum(first_hat)
    second_hat = e_half * state_hat + q_half * react_a
    react_b = react_spectrum(second_hat)
    third_hat = e_half * first_hat + q_half * (2.0 * react_b - react_u)
    react_c = react_spectrum(third_hat)
    new_hat = (
        e_full * state_hat + f_one * react_u + 2.0 * f_two * (react_a + react_b) + f_three * react_c
    )
    return inverse_all(new_hat[None])[0]


def solution(mesh):
    placed = (P(("row", "col"), None, None),)
    return jax.shard_map(
        body, mesh=mesh, in_specs=placed, out_specs=P(("row", "col"), None, None), check_vma=False
    )
```

profile of v0, /device:TPU:0, one launch (start us, length us, event | category | flops | bytes accessed | tf_op | source)
XLA Modules:
  0.0 764.0 jit_solution(2399935068365808978)
XLA Ops:
  4.5 3.5 fusion.127
  14.2 7.3 all-to-all-start.1
  21.6 6.0 fusion.10
  27.7 7.2 fusion.13
  34.9 5.2 copy.81
  40.1 6.1 all-to-all-start
  47.5 7.0 fusion.125
  57.7 83.5 %all-to-all-done = f32[32,2,2,8,8,128]{5,2,3,4,1,0:T(2,128)} async-done(((f32[32,2,2,8,8,128]{5,2,3,4,1,0:T(2,128)}), f32[32,2,2,8,8,128]{5,2,3,4,1,0:T(2,128)}, u32[]{:S(2)}, u32[]{:S(2)}) %all-to-all-start) | async-done | bytes 4194336 | tf_op jit(solution)/shard_map/all_to_all | solution.py:80
  141.2 11.0 %fusion.16 = f32[2,2,8,128,256]{4,3,2,0,1:T(8,128)S(1)} fusion(f32[32,2,2,8,8,128]{5,2,3,4,1,0:T(2,128)} %all-to-all-done, f32[1,1,32,8,256]{4,2,0,3,1:T(8,128)S(1)} %get-tuple-element.21, f32[1,1,32,8,256]{4,2,0,3,1:T(8,128)S(1)} %get-tuple-element.20, f32[1,1,32,8,256]{4,2,0,3,1:T(8,128)S(1)} %get-tuple-element.19), kind=kOutput, calls=%fused_computation.26 | convolution fusion | flops 6443237376 | bytes 9175040 | tf_op jit(solution)/shard_map/sfpmlz,pqsmk->fqlzk/dot_general | solution.py:73
  166.0 5.6 fusion.69
  173.8 6.3 all-to-all-start.2
  191.7 38.0 %all-to-all-done.2 = f32[32,1,2,8,8,128]{5,3,4,2,1,0:T(8,128)} async-done(((f32[32,1,2,8,8,128]{5,3,4,2,1,0:T(8,128)}), f32[32,1,2,8,8,128]{5,3,4,2,1,0:T(8,128)}, u32[]{:S(2)}, u32[]{:S(2)}) %all-to-all-start.2) | async-done | bytes 2097184 | tf_op jit(solution)/shard_map/all_to_all | solution.py:87
  229.7 6.4 fusion.58
  242.1 3.3 fusion.99
  255.8 5.9 fusion.72
  263.8 6.4 all-to-all-start.4
  277.6 42.6 %all-to-all-done.4 = f32[32,1,2,8,8,128]{5,4,3,2,1,0:T(8,128)} async-done(((f32[32,1,2,8,8,128]{5,4,3,2,1,0:T(8,128)}), f32[32,1,2,8,8,128]{5,4,3,2,1,0:T(8,128)}, u32[]{:S(2)}, u32[]{:S(2)}) %all-to-all-start.4) | async-done | bytes 2097184 | tf_op jit(solution)/shard_map/all_to_all | solution.py:80
  320.1 6.3 fusion.75
  336.9 3.2 all-to-all-start.7
  340.1 5.6 fusion.78
  347.2 6.0 all-to-all-start.6
  362.6 40.5 %all-to-all-done.6 = f32[32,1,2,8,8,128]{5,3,4,2,1,0:T(8,128)} async-done(((f32[32,1,2,8,8,128]{5,3,4,2,1,0:T(8,128)}), f32[32,1,2,8,8,128]{5,3,4,2,1,0:T(8,128)}, u32[]{:S(2)}, u32[]{:S(2)}) %all-to-all-start.6) | async-done | bytes 2097184 | tf_op jit(solution)/shard_map/all_to_all | solution.py:87
  403.1 6.4 fusion.48
  415.4 3.3 fusion.102
  426.4 3.3 all-to-all-start.9
  429.7 5.9 fusion.81
  437.1 6.3 all-to-all-start.8
  452.7 40.7 %all-to-all-done.8 = f32[32,1,2,8,8,128]{5,4,3,2,1,0:T(8,128)} async-done(((f32[32,1,2,8,8,128]{5,4,3,2,1,0:T(8,128)}), f32[32,1,2,8,8,128]{5,4,3,2,1,0:T(8,128)}, u32[]{:S(2)}, u32[]{:S(2)}) %all-to-all-start.8) | async-done | bytes 2097184 | tf_op jit(solution)/shard_map/all_to_all | solution.py:80
  493.4 6.3 fusion.84
  499.8 3.3 multiply_add_fusion
  512.2 3.2 all-to-all-start.11
  515.4 5.6 fusion.87
  522.5 6.0 all-to-all-start.10
  537.9 40.5 %all-to-all-done.10 = f32[32,1,2,8,8,128]{5,3,4,2,1,0:T(8,128)} async-done(((f32[32,1,2,8,8,128]{5,3,4,2,1,0:T(8,128)}), f32[32,1,2,8,8,128]{5,3,4,2,1,0:T(8,128)}, u32[]{:S(2)}, u32[]{:S(2)}) %all-to-all-start.10) | async-done | bytes 2097184 | tf_op jit(solution)/shard_map/all_to_all | solution.py:87
  578.4 6.4 fusion.38
  590.7 3.7 fusion.105
  594.4 2.8 fusion.144
  602.3 3.2 all-to-all-start.13
  605.5 5.9 fusion.90
  612.9 5.9 all-to-all-start.12
  628.1 40.7 %all-to-all-done.12 = f32[32,1,2,8,8,128]{5,4,3,2,1,0:T(8,128)} async-done(((f32[32,1,2,8,8,128]{5,4,3,2,1,0:T(8,128)}), f32[32,1,2,8,8,128]{5,4,3,2,1,0:T(8,128)}, u32[]{:S(2)}, u32[]{:S(2)}) %all-to-all-start.12) | async-done | bytes 2097184 | tf_op jit(solution)/shard_map/all_to_all | solution.py:80
  668.8 6.3 fusion.93
  675.1 4.1 fusion.9
  691.0 4.0 fusion.96
  698.2 4.5 all-to-all-start.14
  704.3 48.3 %all-to-all-done.14 = f32[32,1,2,8,8,128]{5,3,4,2,1,0:T(8,128)} async-done(((f32[32,1,2,8,8,128]{5,3,4,2,1,0:T(8,128)}), f32[32,1,2,8,8,128]{5,3,4,2,1,0:T(8,128)}, u32[]{:S(2)}, u32[]{:S(2)}) %all-to-all-start.14) | async-done | bytes 2097184 | tf_op jit(solution)/shard_map/all_to_all | solution.py:87
  752.7 6.1 fusion.28
  760.6 3.2 bitcast_add_fusion
  (251 shorter events, 173.8 us)
Async XLA Ops:
  1.1 20.5 %copy-start.37 = (f32[1,256,256]{1,2,0:T(8,128)}, f32[1,256,256]{1,2,0:T(8,128)S(1)}, u32[]{:S(2)}) copy-start(f32[1,256,256]{1,2,0:T(8,128)S(1)} %get-tuple-element.25) | copy-start | bytes 786436
  1.1 20.5 %copy-start.38 = (f32[1,256,256]{1,2,0:T(8,128)}, f32[1,256,256]{1,2,0:T(8,128)S(1)}, u32[]{:S(2)}) copy-start(f32[1,256,256]{1,2,0:T(8,128)S(1)} %get-tuple-element.26) | copy-start | bytes 786436
  2.2 5.9 copy-start.39
  9.9 17.7 %copy-start.3 = (f32[2,2,256,32,8,1]{2,3,0,1,4,5:T(8,128)}, f32[2,2,256,32,8,1]{2,3,0,1,4,5:T(8,128)S(1)}, u32[]{:S(2)}) copy-start(f32[2,2,256,32,8,1]{2,3,0,1,4,5:T(8,128)S(1)} %get-tuple-element.8) | copy-start | bytes 3145732
  14.2 25.9 %all-to-all-start.1 = ((f32[32,1,256]{2,1,0:T(1,128)}), f32[32,1,256]{2,1,0:T(1,128)S(1)}, u32[]{:S(2)}, u32[]{:S(2)}) async-start(f32[32,1,256]{2,1,0:T(1,128)} %reshape.866), calls=%async_computation.1 | async-start | bytes 65536 | tf_op jit(solution)/shard_map/all_to_all | solution.py:81
  21.6 6.1 copy-start.28
  21.6 6.1 copy-start.40
  40.1 101.1 %all-to-all-start = ((f32[32,2,2,8,8,128]{5,2,3,4,1,0:T(2,128)}), f32[32,2,2,8,8,128]{5,2,3,4,1,0:T(2,128)}, u32[]{:S(2)}, u32[]{:S(2)}) async-start(f32[32,2,2,8,8,128]{5,2,3,4,1,0:T(2,128)} %copy.81), calls=%async_computation | async-start | bytes 8388608 | tf_op jit(solution)/shard_map/all_to_all | solution.py:80
  47.5 93.7 %copy-start.24 = (f32[1,1,32,8,256]{4,2,0,3,1:T(8,128)}, f32[1,1,32,8,256]{4,2,0,3,1:T(8,128)S(1)}, u32[]{:S(2)}) copy-start(f32[1,1,32,8,256]{4,2,0,3,1:T(8,128)S(1)} %get-tuple-element.20) | copy-start | bytes 786436
  47.5 93.7 %copy-start.26 = (f32[1,1,32,8,256]{4,2,0,3,1:T(8,128)}, f32[1,1,32,8,256]{4,2,0,3,1:T(8,128)S(1)}, u32[]{:S(2)}) copy-start(f32[1,1,32,8,256]{4,2,0,3,1:T(8,128)S(1)} %get-tuple-element.21) | copy-start | bytes 786436
  141.2 11.1 %copy-start.12 = (f32[8,129,256]{2,1,0:T(8,128)S(1)}, f32[8,129,256]{2,1,0:T(8,128)}, u32[]{:S(2)}) copy-start(f32[8,129,256]{2,1,0:T(8,128)} %get-tuple-element.14) | copy-start | bytes 3170308
  141.2 11.1 %copy-start.14 = (f32[8,129,256]{2,1,0:T(8,128)S(1)}, f32[8,129,256]{2,1,0:T(8,128)}, u32[]{:S(2)}) copy-start(f32[8,129,256]{2,1,0:T(8,128)} %get-tuple-element.18) | copy-start | bytes 3170308
  141.2 11.1 %copy-start.41 = (f32[2,2,8,1,256]{4,3,2,0,1:T(1,128)S(1)}, f32[2,2,8,1,256]{4,3,2,0,1:T(1,128)}, u32[]{:S(2)}) copy-start(f32[2,2,8,1,256]{4,3,2,0,1:T(1,128)} %reshape_bitcast_fusion) | copy-start | bytes 98308
  163.5 9.7 %all-to-all-start.3 = ((f32[32,1,128]{2,1,0:T(1,128)}), f32[32,1,128]{2,1,0:T(1,128)S(1)}, u32[]{:S(2)}, u32[]{:S(2)}) async-start(f32[32,1,128]{2,1,0:T(1,128)} %reshape.868), calls=%async_computation.3 | async-start | bytes 32768 | tf_op jit(solution)/shard_map/all_to_all | solution.py:88
  173.8 55.9 %all-to-all-start.2 = ((f32[32,1,2,8,8,128]{5,3,4,2,1,0:T(8,128)}), f32[32,1,2,8,8,128]{5,3,4,2,1,0:T(8,128)}, u32[]{:S(2)}, u32[]{:S(2)}) async-start(f32[32,1,2,8,8,128]{5,3,4,2,1,0:T(8,128)} %copy.89), calls=%async_computation.2 | async-start | bytes 4194304 | tf_op jit(solution)/shard_map/all_to_all | solution.py:87
  229.7 6.4 copy-start.33
  229.7 6.4 copy-start.59
  253.2 10.0 %all-to-all-start.5 = ((f32[32,1,128]{2,1,0:T(1,128)}), f32[32,1,128]{2,1,0:T(1,128)S(1)}, u32[]{:S(2)}, u32[]{:S(2)}) async-start(f32[32,1,128]{2,1,0:T(1,128)} %reshape.870), calls=%async_computation.5 | async-start | bytes 32768 | tf_op jit(solution)/shard_map/all_to_all | solution.py:81
  263.8 56.4 %all-to-all-start.4 = ((f32[32,1,2,8,8,128]{5,4,3,2,1,0:T(8,128)}), f32[32,1,2,8,8,128]{5,4,3,2,1,0:T(8,128)}, u32[]{:S(2)}, u32[]{:S(2)}) async-start(f32[32,1,2,8,8,128]{5,4,3,2,1,0:T(8,128)} %copy.99), calls=%async_computation.4 | async-start | bytes 4194304 | tf_op jit(solution)/shard_map/all_to_all | solution.py:80
  320.1 6.3 copy-start.13
  320.1 6.3 copy-start.15
  336.9 10.3 %all-to-all-start.7 = ((f32[32,1,128]{2,1,0:T(1,128)}), f32[32,1,128]{2,1,0:T(1,128)}, u32[]{:S(2)}, u32[]{:S(2)}) async-start(f32[32,1,128]{2,1,0:T(1,128)} %reshape.872), calls=%async_computation.7 | async-start | bytes 32768 | tf_op jit(solution)/shard_map/all_to_all | solution.py:88
  347.2 55.9 %all-to-all-start.6 = ((f32[32,1,2,8,8,128]{5,3,4,2,1,0:T(8,128)}), f32[32,1,2,8,8,128]{5,3,4,2,1,0:T(8,128)}, u32[]{:S(2)}, u32[]{:S(2)}) async-start(f32[32,1,2,8,8,128]{5,3,4,2,1,0:T(8,128)} %copy.108), calls=%async_computation.6 | async-start | bytes 4194304 | tf_op jit(solution)/shard_map/all_to_all | solution.py:87
  403.1 6.4 copy-start.34
  403.1 6.4 copy-start.60
  426.4 10.7 %all-to-all-start.9 = ((f32[32,1,128]{2,1,0:T(1,128)}), f32[32,1,128]{2,1,0:T(1,128)}, u32[]{:S(2)}, u32[]{:S(2)}) async-start(f32[32,1,128]{2,1,0:T(1,128)} %reshape.874), calls=%async_computation.9 | async-start | bytes 32768 | tf_op jit(solution)/shard_map/all_to_all | solution.py:81
  437.1 56.3 %all-to-all-start.8 = ((f32[32,1,2,8,8,128]{5,4,3,2,1,0:T(8,128)}), f32[32,1,2,8,8,128]{5,4,3,2,1,0:T(8,128)}, u32[]{:S(2)}, u32[]{:S(2)}) async-start(f32[32,1,2,8,8,128]{5,4,3,2,1,0:T(8,128)} %copy.118), calls=%async_computation.8 | async-start | bytes 4194304 | tf_op jit(solution)/shard_map/all_to_all | solution.py:80
  493.4 6.3 copy-start.1
  493.4 6.3 copy-start.42
  493.4 6.3 copy-start.44
  512.2 10.3 %all-to-all-start.11 = ((f32[32,1,128]{2,1,0:T(1,128)}), f32[32,1,128]{2,1,0:T(1,128)}, u32[]{:S(2)}, u32[]{:S(2)}) async-start(f32[32,1,128]{2,1,0:T(1,128)} %reshape.876), calls=%async_computation.11 | async-start | bytes 32768 | tf_op jit(solution)/shard_map/all_to_all | solution.py:88
  522.5 55.9 %all-to-all-start.10 = ((f32[32,1,2,8,8,128]{5,3,4,2,1,0:T(8,128)}), f32[32,1,2,8,8,128]{5,3,4,2,1,0:T(8,128)}, u32[]{:S(2)}, u32[]{:S(2)}) async-start(f32[32,1,2,8,8,128]{5,3,4,2,1,0:T(8,128)} %copy.127), calls=%async_computation.10 | async-start | bytes 4194304 | tf_op jit(solution)/shard_map/all_to_all | solution.py:87
  578.4 6.4 copy-start.35
  578.4 6.4 copy-start.61
  602.3 10.6 %all-to-all-start.13 = ((f32[32,1,128]{2,1,0:T(1,128)}), f32[32,1,128]{2,1,0:T(1,128)}, u32[]{:S(2)}, u32[]{:S(2)}) async-start(f32[32,1,128]{2,1,0:T(1,128)} %reshape.878), calls=%async_computation.13 | async-start | bytes 32768 | tf_op jit(solution)/shard_map/all_to_all | solution.py:81
  612.9 55.9 %all-to-all-start.12 = ((f32[32,1,2,8,8,128]{5,4,3,2,1,0:T(8,128)}), f32[32,1,2,8,8,128]{5,4,3,2,1,0:T(8,128)}, u32[]{:S(2)}, u32[]{:S(2)}) async-start(f32[32,1,2,8,8,128]{5,4,3,2,1,0:T(8,128)} %copy.137), calls=%async_computation.12 | async-start | bytes 4194304 | tf_op jit(solution)/shard_map/all_to_all | solution.py:80
  668.8 6.3 copy-start.2
  668.8 6.3 copy-start.43
  668.8 6.3 copy-start.45
  668.8 6.3 copy-start.48
  675.1 5.5 copy-start.7
  680.7 10.3 %copy-start.23 = (f32[1,2,8,129,256]{4,3,2,0,1:T(8,128)S(1)}, f32[1,2,8,129,256]{4,3,2,0,1:T(8,128)}, u32[]{:S(2)}) copy-start(f32[1,2,8,129,256]{4,3,2,0,1:T(8,128)} %copy-done.22) | copy-start | bytes 6340612
  688.5 9.7 %all-to-all-start.15 = ((f32[32,1,128]{2,1,0:T(1,128)}), f32[32,1,128]{2,1,0:T(1,128)S(1)}, u32[]{:S(2)}, u32[]{:S(2)}) async-start(f32[32,1,128]{2,1,0:T(1,128)} %reshape.880), calls=%async_computation.15 | async-start | bytes 32768 | tf_op jit(solution)/shard_map/all_to_all | solution.py:88
  696.5 7.2 copy-start.25
  696.5 7.2 copy-start.27
  698.2 54.5 %all-to-all-start.14 = ((f32[32,1,2,8,8,128]{5,3,4,2,1,0:T(8,128)}), f32[32,1,2,8,8,128]{5,3,4,2,1,0:T(8,128)}, u32[]{:S(2)}, u32[]{:S(2)}) async-start(f32[32,1,2,8,8,128]{5,3,4,2,1,0:T(8,128)} %copy.146), calls=%async_computation.14 | async-start | bytes 4194304 | tf_op jit(solution)/shard_map/all_to_all | solution.py:87
  704.3 54.4 %copy-start.36 = (f32[2,256,256]{1,2,0:T(8,128)S(1)}, f32[2,256,256]{1,2,0:T(8,128)}, u32[]{:S(2)}) copy-start(f32[2,256,256]{1,2,0:T(8,128)} %copy-done.32) | copy-start | bytes 1572868
  704.3 54.4 %copy-start.62 = (f32[128]{0:T(128)S(1)}, f32[128]{0:T(128)}, u32[]{:S(2)}) copy-start(f32[128]{0:T(128)} %compare_select_fusion) | copy-start | bytes 1540
  (31 other events, 68.4 us)
where the time goes:
time: 774 us; the launch traced here: 764 us
  waiting for transfers between devices  377 us (49%)
  matrix products  177 us (23%)
  local copies, waits for them, and re-layouts  96.2 us (12%)
  starting transfers between devices  75.1 us (10%)
  other arithmetic  37.5 us (5%)
    all_to_all x4, waiting for transfers between devices, spectra_move(): lax.all_to_all(lower, ('row', 'col'), split_axis=0, concat_axis=0, tiled=...  207 us
    dot_general x48, matrix products, contract(): jnp.einsum(form, left, right, precision=lax.Precision.HIGHEST, preferred_...  177 us
    all_to_all x4, waiting for transfers between devices, fields_move(): lax.all_to_all(lower, ('row', 'col'), split_axis=0, concat_axis=0, tiled=...  167 us
    unnamed x149, local copies, waits for them, and re-layouts  44.1 us
    all_to_all x4, starting transfers between devices, spectra_move(): lax.all_to_all(lower, ('row', 'col'), split_axis=0, concat_axis=0, tiled=...  24.7 us
    all_to_all x4, starting transfers between devices, fields_move(): lax.all_to_all(lower, ('row', 'col'), split_axis=0, concat_axis=0, tiled=...  22.8 us
    another operation x14, local copies, waits for them, and re-layouts  20.4 us
    transpose x13, local copies, waits for them, and re-layouts, contract(): jnp.einsum(form, left, right, precision=lax.Precision.HIGHEST, preferred_...  18.2 us
  transfers between devices with their start and end apart: 16, of which 10 were waited for; matrix products, arithmetic and copies ran while one was open for 18% of the time, Pallas kernels for 0%

commit v1 on v0

v1 whole, which is shorter than its diff:
```python
import functools
import math

import jax
import jax.numpy as jnp
import numpy as np
from jax import lax
from jax.experimental import pallas as pl
from jax.experimental.pallas import tpu as pltpu
from jax.sharding import PartitionSpec as P

growth_rate = 0.3
quadratic = 1.0
time_step = 0.2
wave_scale = 4.0


def wavenumbers(count, offset, length):
    indices = offset + jnp.arange(count)
    signed = jnp.where(indices * 2 < length, indices, indices - length)
    return wave_scale * signed.astype(jnp.float32) / length


def phi_values(argument):
    within = jnp.abs(argument) < 1.0
    inside = jnp.where(within, argument, 0.0)
    outside = jnp.where(within, 2.0, argument)
    series = []
    for degree in (1, 2, 3):
        running = jnp.zeros_like(argument) + 1.0 / math.factorial(11 + degree)
        for exponent in range(10, -1, -1):
            running = running * inside + 1.0 / math.factorial(exponent + degree)
        series.append(running)
    growth_term = jnp.exp(outside)
    closed_one = (growth_term - 1.0) / outside
    closed_two = (growth_term - 1.0 - outside) / (outside * outside)
    closed_three = (growth_term - 1.0 - outside - 0.5 * outside * outside) / (
        outside * outside * outside
    )
    return (
        jnp.where(within, series[0], closed_one),
        jnp.where(within, series[1], closed_two),
        jnp.where(within, series[2], closed_three),
    )


def step_factors(ksq):
    lin = growth_rate - (1.0 - ksq) * (1.0 - ksq)
    scaled = time_step * lin
    half_phi, _, _ = phi_values(0.5 * scaled)
    first_phi, second_phi, third_phi = phi_values(scaled)
    e_half = jnp.exp(0.5 * scaled)
    q_half = 0.5 * time_step * half_phi
    e_full = jnp.exp(scaled)
    f_one = time_step * (first_phi - 3.0 * second_phi + 4.0 * third_phi)
    f_two = time_step * (second_phi - 2.0 * third_phi)
    f_three = time_step * (4.0 * third_phi - second_phi)
    return (e_half, q_half, e_full, f_one, f_two, f_three)


def reaction(values):
    return quadratic * values * values - values * values * values


def cas_table(length):
    modes = jnp.arange(length, dtype=jnp.int32)
    product = jnp.mod(modes[:, None] * modes[None, :], length)
    angle = 2.0 * math.pi / length * product.astype(jnp.float32)
    return (jnp.cos(angle) + jnp.sin(angle)) / math.sqrt(length)


def contract(form, left, right):
    return jnp.einsum(
        form, left, right, precision=lax.Precision.HIGHEST, preferred_element_type=jnp.float32
    )


def move(blocks):
    return lax.all_to_all(blocks, ("row", "col"), split_axis=0, concat_axis=0, tiled=True)


def plain_body(initial_field):
    devices_all = lax.axis_size("row") * lax.axis_size("col")
    rows_x, size_y, size_z = initial_field.shape
    size_x = rows_x * devices_all
    share_y = size_y // devices_all
    table_z = cas_table(size_z)
    table_y = cas_table(size_y).reshape((devices_all, share_y, size_y))
    table_x = cas_table(size_x).reshape((devices_all, rows_x, size_x))
    offset = lax.axis_index(("row", "col")) * share_y
    wave_y = wavenumbers(share_y, offset, size_y)
    wave_z = wavenumbers(size_z, 0, size_z)
    wave_x = wavenumbers(size_x, 0, size_x)
    ksq = wave_y[:, None, None] ** 2 + wave_z[None, None, :] ** 2 + wave_x[None, :, None] ** 2
    e_half, q_half, e_full, f_one, f_two, f_three = step_factors(ksq)

    def forward_all(values):
        over_z = contract("xyn,nk->xyk", values, table_z)
        over_y = contract("sly,xyk->slxk", table_y, over_z)
        return contract("sxX,slxk->lXk", table_x, move(over_y))

    def inverse_all(spectra):
        over_x = contract("sxX,lXk->slxk", table_x, spectra)
        over_y = contract("slxk,sly->xyk", move(over_x), table_y)
        return contract("xyk,kn->xyn", over_y, table_z)

    def react_spectrum(spectrum):
        return forward_all(reaction(inverse_all(spectrum)))

    state_hat = forward_all(initial_field)
    react_u = forward_all(reaction(initial_field))
    first_hat = e_half * state_hat + q_half * react_u
    react_a = react_spectrum(first_hat)
    second_hat = e_half * state_hat + q_half * react_a
    react_b = react_spectrum(second_hat)
    third_hat = e_half * first_hat + q_half * (2.0 * react_b - react_u)
    react_c = react_spectrum(third_hat)
    new_hat = (
        e_full * state_hat + f_one * react_u + 2.0 * f_two * (react_a + react_b) + f_three * react_c
    )
    return inverse_all(new_hat)


LANES = 128


def split_table(length):
    modes = np.arange(length)
    angle = 2.0 * np.pi / length * ((modes[:, None] * modes[None, :]) % length)
    table = ((np.cos(angle) + np.sin(angle)) / np.sqrt(length)).astype(np.float32)
    upper = table.astype(jnp.bfloat16)
    lower = (table - upper.astype(np.float32)).astype(jnp.bfloat16)
    return upper, lower


def split_values(values):
    upper = values.astype(jnp.bfloat16)
    lower = (values - upper.astype(jnp.float32)).astype(jnp.bfloat16)
    return upper, lower


def kernel(
    count, columns, rows_x, share_y, size_x, size_y, size_z,
    field, left, right, out,
    send_f, got_f, send_i, got_i, held, third, total,
    e_half, q_half, e_full, f_one, f_two, f_three,
    sent_f, came_f, sent_i, came_i,
):
    me = lax.axis_index("row") * columns + lax.axis_index("col")
    block = rows_x * share_y
    halves = size_z // LANES
    pairs = share_y // 2
    group = 2 if rows_x % 2 == 0 else 1

    def mul_left(values):
        upper, lower = split_values(values)
        stacked = jnp.concatenate([upper, lower, upper], axis=0)
        return jnp.dot(left[...], stacked, preferred_element_type=jnp.float32)

    def mul_right(values):
        upper, lower = split_values(values)
        stacked = jnp.concatenate([upper, lower, upper], axis=1)
        return jnp.dot(stacked, right[...], preferred_element_type=jnp.float32)

    def send_forward(index, half, start, length):
        buffer = index % 2
        here = pl.multiple_of(me * block + start, 8)
        mine = got_f.at[buffer, half, pl.ds(here, length), :]
        pltpu.make_async_copy(
            send_f.at[buffer, half, me, pl.ds(start, length), :], mine, came_f.at[index, half]
        ).start()

        def one(offset, carry):
            other = (me + offset) % count
            pltpu.make_async_remote_copy(
                src_ref=send_f.at[buffer, half, other, pl.ds(start, length), :],
                dst_ref=mine,
                send_sem=sent_f.at[index, half],
                recv_sem=came_f.at[index, half],
                device_id=(other // columns, other % columns),
                device_id_type=pl.DeviceIdType.MESH,
            ).start()
            return carry

        lax.fori_loop(1, count, one, 0)

    def send_inverse(index, half):
        mine = got_i.at[half, me]

        def rows(device):
            return send_i.at[half, pl.ds(pl.multiple_of(device * block, 8), block), :]

        pltpu.make_async_copy(rows(me), mine, came_i.at[index, half]).start()

        def one(offset, carry):
            other = (me + offset) % count
            pltpu.make_async_remote_copy(
                src_ref=rows(other),
                dst_ref=mine,
                send_sem=sent_i.at[index, half],
                recv_sem=came_i.at[index, half],
                device_id=(other // columns, other % columns),
                device_id_type=pl.DeviceIdType.MESH,
            ).start()
            return carry

        lax.fori_loop(1, count, one, 0)

    def wait_bytes(ref, sem):
        pltpu.make_async_copy(ref, ref, sem).wait()

    def wait_sent_forward(index):
        for half in range(halves):
            wait_bytes(send_f.at[index % 2, half, pl.ds(0, count - 1)], sent_f.at[index, half])

    def wait_sent_inverse(index, half):
        wait_bytes(send_i.at[half, pl.ds(0, (count - 1) * block), :], sent_i.at[index, half])

    def forward(index, source):
        def plane(m):
            spectrum = mul_left(mul_right(source(m)))
            rows = pl.ds(pl.multiple_of(m * share_y, 8), share_y)
            for half in range(halves):
                part = spectrum[:, half * LANES : (half + 1) * LANES]
                send_f[index % 2, half, :, rows, :] = part.reshape(count, share_y, LANES)

        def step(g, carry):
            for inner in range(group):
                plane(g * group + inner)
            send_forward(
                index, 0, pl.multiple_of(g * group * share_y, 8), group * share_y
            )
            return carry

        lax.fori_loop(0, rows_x // group, step, 0)
        for half in range(1, halves):
            send_forward(index, half, 0, block)

    def physical(m):
        rows = pl.ds(pl.multiple_of(m * share_y, 8), share_y)
        parts = [got_i[half, :, rows, :].reshape(size_y, LANES) for half in range(halves)]
        return mul_right(mul_left(jnp.concatenate(parts, axis=1)))

    def spectrum_at(index, half, pair):
        parts = [
            got_f[index % 2, half, pl.ds(pair * 2 + inner, size_x, stride=share_y), :]
            for inner in range(2)
        ]
        return mul_left(jnp.concatenate(parts, axis=1))

    def arrived_forward(index, half):
        wait_bytes(got_f.at[index % 2, half], came_f.at[index, half])

    def inverse(index, source, update):
        for half in range(halves):
            arrived_forward(source, half)
            if index > 0:
                wait_sent_inverse(index - 1, half)

            def step(pair, carry):
                values = mul_left(update(half, pair, spectrum_at(source, half, pair)))
                for inner in range(2):
                    send_i[half, pl.ds(pair * 2 + inner, size_x, stride=share_y), :] = values[
                        :, inner * LANES : (inner + 1) * LANES
                    ]
                return carry

            lax.fori_loop(0, pairs, step, 0)
            send_inverse(index, half)

    def arrived_inverse(index):
        for half in range(halves):
            wait_bytes(got_i.at[half], came_i.at[index, half])

    def wave(indices, length):
        signed = jnp.where(indices * 2 < length, indices, indices - length)
        return wave_scale * signed.astype(jnp.float32) / length

    forward(0, lambda m: field[m])
    forward(1, lambda m: reaction(field[m]))

    rows_step = 32

    def factors(item, carry):
        half = item // (pairs * (size_x // rows_step))
        rest = item % (pairs * (size_x // rows_step))
        pair = rest // (size_x // rows_step)
        start = pl.multiple_of(rest % (size_x // rows_step) * rows_step, 8)
        dims = (rows_step, 2 * LANES)
        lane = lax.broadcasted_iota(jnp.int32, dims, 1)
        second = (lane >= LANES).astype(jnp.int32)
        index_z = lane - second * LANES + half * LANES
        index_y = second + (me * share_y + pair * 2)
        index_x = lax.broadcasted_iota(jnp.int32, dims, 0) + start
        wave_y, wave_z, wave_x = wave(index_y, size_y), wave(index_z, size_z), wave(index_x, size_x)
        ksq = wave_y * wave_y + wave_z * wave_z + wave_x * wave_x
        values = step_factors(ksq)
        where = pl.ds(start, rows_step)
        for ref, value in zip((e_half, q_half, e_full, f_one, f_two, f_three), values):
            ref[half, pair, where, :] = value
        return carry

    lax.fori_loop(0, halves * pairs * (size_x // rows_step), factors, 0)

    for half in range(halves):
        arrived_forward(0, half)

        def keep(pair, carry):
            total[half, pair] = spectrum_at(0, half, pair)
            return carry

        lax.fori_loop(0, pairs, keep, 0)

    def update_first(half, pair, react_u):
        state_hat = total[half, pair]
        base = e_half[half, pair] * state_hat
        gain = q_half[half, pair] * react_u
        first_hat = base + gain
        held[half, pair] = base
        third[half, pair] = e_half[half, pair] * first_hat - gain
        total[half, pair] = e_full[half, pair] * state_hat + f_one[half, pair] * react_u
        return first_hat

    def update_second(half, pair, react_a):
        total[half, pair] = total[half, pair] + 2.0 * f_two[half, pair] * react_a
        return held[half, pair] + q_half[half, pair] * react_a

    def update_third(half, pair, react_b):
        total[half, pair] = total[half, pair] + 2.0 * f_two[half, pair] * react_b
        return third[half, pair] + 2.0 * q_half[half, pair] * react_b

    def update_last(half, pair, react_c):
        return total[half, pair] + f_three[half, pair] * react_c

    updates = (update_first, update_second, update_third, update_last)
    for index, update in enumerate(updates):
        inverse(index, index + 1, update)
        if index < 3:
            wait_sent_forward(index)
            arrived_inverse(index)
            forward(index + 2, lambda m: reaction(physical(m)))
    for index in (3, 4):
        wait_sent_forward(index)
    arrived_inverse(3)

    def finish(m, carry):
        out[m] = physical(m)
        return carry

    lax.fori_loop(0, rows_x, finish, 0)
    for half in range(halves):
        wait_sent_inverse(3, half)


def body(initial_field):
    rows_x, size_y, size_z = initial_field.shape
    columns = lax.axis_size("col")
    count = lax.axis_size("row") * columns
    size_x = rows_x * count
    share_y = size_y // count
    fits = share_y % 8 == 0 and size_z % LANES == 0 and size_x == size_y == size_z
    if not fits:
        return plain_body(initial_field)
    upper, lower = split_table(size_x)
    left = np.concatenate([upper, upper, lower], axis=1)
    right = np.concatenate([upper, upper, lower], axis=0)
    halves, pairs, block = size_z // LANES, share_y // 2, rows_x * share_y
    spectral = pltpu.VMEM((halves, pairs, size_x, 2 * LANES), jnp.float32)
    vmem = pl.BlockSpec(memory_space=pltpu.VMEM)
    return pl.pallas_call(
        functools.partial(
            kernel, count, columns, rows_x, share_y, size_x, size_y, size_z
        ),
        out_shape=jax.ShapeDtypeStruct(initial_field.shape, jnp.float32),
        in_specs=[vmem] * 3,
        out_specs=vmem,
        scratch_shapes=[
            pltpu.VMEM((2, halves, count, block, LANES), jnp.float32),
            pltpu.VMEM((2, halves, count * block, LANES), jnp.float32),
            pltpu.VMEM((halves, count * block, LANES), jnp.float32),
            pltpu.VMEM((halves, count, block, LANES), jnp.float32),
        ]
        + [spectral] * 9
        + [
            pltpu.SemaphoreType.DMA((5, halves)),
            pltpu.SemaphoreType.DMA((5, halves)),
            pltpu.SemaphoreType.DMA((4, halves)),
            pltpu.SemaphoreType.DMA((4, halves)),
        ],
        compiler_params=pltpu.CompilerParams(
            has_side_effects=True, vmem_limit_bytes=60 * 1024 * 1024
        ),
    )(initial_field, jnp.asarray(left), jnp.asarray(right))


def solution(mesh):
    placed = (P(("row", "col"), None, None),)
    return jax.shard_map(
        body, mesh=mesh, in_specs=placed, out_specs=P(("row", "col"), None, None), check_vma=False
    )
```

time: 774 us -> 439 us (0.57); the launches traced: 764 us -> 439 us
  Pallas kernels: 0 us -> 436 us
  waiting for transfers between devices: 377 us -> 0 us
  matrix products: 177 us -> 0 us
  local copies, waits for them, and re-layouts: 96.2 us -> 3.05 us
  starting transfers between devices: 75.1 us -> 0 us
  other arithmetic: 37.5 us -> 0 us
    pallas_call x0 -> x1, Pallas kernels: none -> 436 us  [body(): pl.pallas_call(functools.partial(kernel, count, columns, rows_x, share_y,...]
    all_to_all x16 -> x0, waiting for transfers between devices: 377 us -> none  [the longest x4 207 us: spectra_move(): lax.all_to_all(lower, ('row', 'col'), split_axis=0, concat_axis=0, tiled=...]
    dot_general x48 -> x0, matrix products: 177 us -> none  [contract(): jnp.einsum(form, left, right, precision=lax.Precision.HIGHEST, preferred_...]
    all_to_all x16 -> x0, starting transfers between devices: 75.1 us -> none  [the longest x4 24.7 us: spectra_move(): lax.all_to_all(lower, ('row', 'col'), split_axis=0, concat_axis=0, tiled=...]
    unnamed x149 -> x1, local copies, waits for them, and re-layouts: 44.1 us -> 3.05 us
    another operation x14 -> x0, local copies, waits for them, and re-layouts: 20.4 us -> none
    transpose x13 -> x0, local copies, waits for them, and re-layouts: 18.2 us -> none  [contract(): jnp.einsum(form, left, right, precision=lax.Precision.HIGHEST, preferred_...]
    all_to_all x8 -> x0, other arithmetic: 12.1 us -> none  [the longest x4 6.06 us: spectra_move(): lax.all_to_all(upper, ('row', 'col'), split_axis=0, concat_axis=0, tiled=...]
  transfers between devices with their start and end apart: 16 -> 0, of which waited for: 10 -> 0; matrix products, arithmetic and copies ran while one was open for 18% -> 0% of each run, Pallas kernels for 0% -> 0%
where the time goes in v1:
time: 439 us
  Pallas kernels  436 us (99%)
    pallas_call x1, Pallas kernels, body(): pl.pallas_call(functools.partial(kernel, count, columns, rows_x, share_y,...  436 us

profile of v1, /device:TPU:0, one launch (start us, length us, event | category | flops | bytes accessed | tf_op | source)
XLA Modules:
  0.0 438.7 jit_solution(8701888499010745205)
XLA Ops:
  0.0 435.7 %shard_map.37 = f32[8,256,256]{2,1,0:T(8,128)} custom-call(f32[8,256,256]{2,1,0:T(8,128)} %field.1, bf16[256,768]{1,0:T(8,128)(2,1)} %constant.4.clone.left, bf16[768,256]{1,0:T(8,128)(2,1)} %constant.5.clone.right), custom_call_target="tpu_custom_call" | custom-call | tf_op jit(solution)/shard_map/pallas_call | solution.py:370
  435.7 3.0 copy.5

commit v2 on v1

--- a/solution.py
+++ b/solution.py
@@ -151,6 +151,8 @@
     halves = size_z // LANES
     pairs = share_y // 2
     group = 2 if rows_x % 2 == 0 else 1
+    parts = rows_x // group
+    early = parts // 2
 
     def mul_left(values):
         upper, lower = split_values(values)
@@ -184,13 +186,15 @@
 
         lax.fori_loop(1, count, one, 0)
 
-    def send_inverse(index, half):
-        mine = got_i.at[half, me]
+    def send_inverse(index, half, part):
+        length = group * share_y
+        mine = got_i.at[half, me, pl.ds(part * length, length), :]
 
         def rows(device):
-            return send_i.at[half, pl.ds(pl.multiple_of(device * block, 8), block), :]
-
-        pltpu.make_async_copy(rows(me), mine, came_i.at[index, half]).start()
+            start = pl.multiple_of(device * block + part * length, 8)
+            return send_i.at[half, pl.ds(start, length), :]
+
+        pltpu.make_async_copy(rows(me), mine, came_i.at[index, part]).start()
 
         def one(offset, carry):
             other = (me + offset) % count
@@ -198,7 +202,7 @@
                 src_ref=rows(other),
                 dst_ref=mine,
                 send_sem=sent_i.at[index, half],
-                recv_sem=came_i.at[index, half],
+                recv_sem=came_i.at[index, part],
                 device_id=(other // columns, other % columns),
                 device_id_type=pl.DeviceIdType.MESH,
             ).start()
@@ -216,7 +220,7 @@
     def wait_sent_inverse(index, half):
         wait_bytes(send_i.at[half, pl.ds(0, (count - 1) * block), :], sent_i.at[index, half])
 
-    def forward(index, source):
+    def forward(index, source, before=None):
         def plane(m):
             spectrum = mul_left(mul_right(source(m)))
             rows = pl.ds(pl.multiple_of(m * share_y, 8), share_y)
@@ -225,6 +229,8 @@
                 send_f[index % 2, half, :, rows, :] = part.reshape(count, share_y, LANES)
 
         def step(g, carry):
+            if before is not None:
+                before(g)
             for inner in range(group):
                 plane(g * group + inner)
             send_forward(
@@ -266,11 +272,16 @@
                 return carry
 
             lax.fori_loop(0, pairs, step, 0)
-            send_inverse(index, half)
-
-    def arrived_inverse(index):
-        for half in range(halves):
-            wait_bytes(got_i.at[half], came_i.at[index, half])
+            for part in range(early):
+                send_inverse(index, half, part)
+        for part in range(early, parts):
+            for half in range(halves):
+                send_inverse(index, half, part)
+
+    def arrived_inverse(index, part):
+        length = group * share_y
+        rows = pl.ds(pl.multiple_of(part * length, 8), length)
+        wait_bytes(got_i.at[:, :, rows, :], came_i.at[index, part])
 
     def wave(indices, length):
         signed = jnp.where(indices * 2 < length, indices, indices - length)
@@ -337,17 +348,21 @@
         inverse(index, index + 1, update)
         if index < 3:
             wait_sent_forward(index)
-            arrived_inverse(index)
-            forward(index + 2, lambda m: reaction(physical(m)))
+            forward(
+                index + 2,
+                lambda m: reaction(physical(m)),
+                lambda g, index=index: arrived_inverse(index, g),
+            )
     for index in (3, 4):
         wait_sent_forward(index)
-    arrived_inverse(3)
-
-    def finish(m, carry):
-        out[m] = physical(m)
+
+    def finish(g, carry):
+        arrived_inverse(3, g)
+        for inner in range(group):
+            out[g * group + inner] = physical(g * group + inner)
         return carry
 
-    lax.fori_loop(0, rows_x, finish, 0)
+    lax.fori_loop(0, parts, finish, 0)
     for half in range(halves):
         wait_sent_inverse(3, half)
 
@@ -385,7 +400,7 @@
             pltpu.SemaphoreType.DMA((5, halves)),
             pltpu.SemaphoreType.DMA((5, halves)),
             pltpu.SemaphoreType.DMA((4, halves)),
-            pltpu.SemaphoreType.DMA((4, halves)),
+            pltpu.SemaphoreType.DMA((4, rows_x)),
         ],
         compiler_params=pltpu.CompilerParams(
             has_side_effects=True, vmem_limit_bytes=60 * 1024 * 1024

time: 439 us -> 424 us (0.966)
  Pallas kernels: 436 us -> 421 us
    pallas_call x1, Pallas kernels: 436 us -> 421 us  [body(): pl.pallas_call(functools.partial(kernel, count, columns, rows_x, share_y,...]
where the time goes in v2:
time: 424 us
  Pallas kernels  421 us (99%)
    pallas_call x1, Pallas kernels, body(): pl.pallas_call(functools.partial(kernel, count, columns, rows_x, share_y,...  421 us

profile of v2, /device:TPU:0, one launch (start us, length us, event | category | flops | bytes accessed | tf_op | source)
XLA Modules:
  0.0 424.0 jit_solution(18432202907542723467)
XLA Ops:
  0.0 421.0 %shard_map.37 = f32[8,256,256]{2,1,0:T(8,128)} custom-call(f32[8,256,256]{2,1,0:T(8,128)} %field.1, bf16[256,768]{1,0:T(8,128)(2,1)} %constant.4.clone.left, bf16[768,256]{1,0:T(8,128)(2,1)} %constant.5.clone.right), custom_call_target="tpu_custom_call" | custom-call | tf_op jit(solution)/shard_map/pallas_call | solution.py:385
  421.0 3.0 copy.5

commit v3 on v2

--- a/solution.py
+++ b/solution.py
@@ -164,6 +164,20 @@
         stacked = jnp.concatenate([upper, lower, upper], axis=1)
         return jnp.dot(stacked, right[...], preferred_element_type=jnp.float32)
 
+    barrier = pltpu.get_barrier_semaphore()
+
+    def greet(offset, carry):
+        other = (me + offset) % count
+        pl.semaphore_signal(
+            barrier,
+            inc=1,
+            device_id=(other // columns, other % columns),
+            device_id_type=pl.DeviceIdType.MESH,
+        )
+        return carry
+
+    lax.fori_loop(1, count, greet, 0)
+
     def send_forward(index, half, start, length):
         buffer = index % 2
         here = pl.multiple_of(me * block + start, 8)
@@ -238,7 +252,14 @@
             )
             return carry
 
-        lax.fori_loop(0, rows_x // group, step, 0)
+        first = 0
+        if index == 0:
+            for m in range(group):
+                plane(m)
+            pl.semaphore_wait(barrier, count - 1)
+            send_forward(0, 0, 0, group * share_y)
+            first = 1
+        lax.fori_loop(first, parts, step, 0)
         for half in range(1, halves):
             send_forward(index, half, 0, block)
 
@@ -403,7 +424,7 @@
             pltpu.SemaphoreType.DMA((4, rows_x)),
         ],
         compiler_params=pltpu.CompilerParams(
-            has_side_effects=True, vmem_limit_bytes=60 * 1024 * 1024
+            collective_id=0, has_side_effects=True, vmem_limit_bytes=60 * 1024 * 1024
         ),
     )(initial_field, jnp.asarray(left), jnp.asarray(right))
 

time: 424 us -> 421 us (level)
  no operation moved by 1% of the time
where the time goes in v3:
time: 421 us
  Pallas kernels  418 us (99%)
    pallas_call x1, Pallas kernels, body(): pl.pallas_call(functools.partial(kernel, count, columns, rows_x, share_y,...  418 us

profile of v3, /device:TPU:0, one launch (start us, length us, event | category | flops | bytes accessed | tf_op | source)
XLA Modules:
  0.0 420.7 jit_solution(7382083225256278866)
XLA Ops:
  0.0 417.7 %shard_map.37 = f32[8,256,256]{2,1,0:T(8,128)} custom-call(f32[8,256,256]{2,1,0:T(8,128)} %field.1, bf16[256,768]{1,0:T(8,128)(2,1)} %constant.4.clone.left, bf16[768,256]{1,0:T(8,128)(2,1)} %constant.5.clone.right), custom_call_target="tpu_custom_call" | custom-call | tf_op jit(solution)/shard_map/pallas_call | solution.py:406
  417.7 3.0 copy.5

commit v4 on v3

--- a/solution.py
+++ b/solution.py
@@ -141,16 +141,16 @@
 
 def kernel(
     count, columns, rows_x, share_y, size_x, size_y, size_z,
-    field, left, right, out,
+    field_in, left, right, out_to,
     send_f, got_f, send_i, got_i, held, third, total,
     e_half, q_half, e_full, f_one, f_two, f_three,
-    sent_f, came_f, sent_i, came_i,
+    sent_f, came_f, sent_i, came_i, field, out, plane_in, plane_out,
 ):
     me = lax.axis_index("row") * columns + lax.axis_index("col")
     block = rows_x * share_y
     halves = size_z // LANES
     pairs = share_y // 2
-    group = 2 if rows_x % 2 == 0 else 1
+    group = 1
     parts = rows_x // group
     early = parts // 2
 
@@ -164,6 +164,14 @@
         stacked = jnp.concatenate([upper, lower, upper], axis=1)
         return jnp.dot(stacked, right[...], preferred_element_type=jnp.float32)
 
+    def load(m):
+        return pltpu.make_async_copy(field_in.at[m], field.at[m], plane_in.at[m])
+
+    def store(m):
+        return pltpu.make_async_copy(out.at[m], out_to.at[m], plane_out.at[m])
+
+    for m in range(rows_x):
+        load(m).start()
     barrier = pltpu.get_barrier_semaphore()
 
     def greet(offset, carry):
@@ -255,6 +263,7 @@
         first = 0
         if index == 0:
             for m in range(group):
+                load(m).wait()
                 plane(m)
             pl.semaphore_wait(barrier, count - 1)
             send_forward(0, 0, 0, group * share_y)
@@ -308,7 +317,11 @@
         signed = jnp.where(indices * 2 < length, indices, indices - length)
         return wave_scale * signed.astype(jnp.float32) / length
 
-    forward(0, lambda m: field[m])
+    def loaded(g):
+        for inner in range(group):
+            load(g * group + inner).wait()
+
+    forward(0, lambda m: field[m], loaded)
     forward(1, lambda m: reaction(field[m]))
 
     rows_step = 32
@@ -381,11 +394,14 @@
         arrived_inverse(3, g)
         for inner in range(group):
             out[g * group + inner] = physical(g * group + inner)
+            store(g * group + inner).start()
         return carry
 
     lax.fori_loop(0, parts, finish, 0)
     for half in range(halves):
         wait_sent_inverse(3, half)
+    for m in range(rows_x):
+        store(m).wait()
 
 
 def body(initial_field):
@@ -408,8 +424,8 @@
             kernel, count, columns, rows_x, share_y, size_x, size_y, size_z
         ),
         out_shape=jax.ShapeDtypeStruct(initial_field.shape, jnp.float32),
-        in_specs=[vmem] * 3,
-        out_specs=vmem,
+        in_specs=[pl.BlockSpec(memory_space=pltpu.HBM), vmem, vmem],
+        out_specs=pl.BlockSpec(memory_space=pltpu.HBM),
         scratch_shapes=[
             pltpu.VMEM((2, halves, count, block, LANES), jnp.float32),
             pltpu.VMEM((2, halves, count * block, LANES), jnp.float32),
@@ -422,6 +438,10 @@
             pltpu.SemaphoreType.DMA((5, halves)),
             pltpu.SemaphoreType.DMA((4, halves)),
             pltpu.SemaphoreType.DMA((4, rows_x)),
+            pltpu.VMEM(initial_field.shape, jnp.float32),
+            pltpu.VMEM(initial_field.shape, jnp.float32),
+            pltpu.SemaphoreType.DMA((rows_x,)),
+            pltpu.SemaphoreType.DMA((rows_x,)),
         ],
         compiler_params=pltpu.CompilerParams(
             collective_id=0, has_side_effects=True, vmem_limit_bytes=60 * 1024 * 1024

time: 421 us -> 419 us (level)
  no operation moved by 1% of the time
where the time goes in v4:
time: 419 us
  Pallas kernels  416 us (99%)
    pallas_call x1, Pallas kernels, body(): pl.pallas_call(functools.partial(kernel, count, columns, rows_x, share_y,...  416 us

profile of v4, /device:TPU:0, one launch (start us, length us, event | category | flops | bytes accessed | tf_op | source)
XLA Modules:
  0.0 419.3 jit_solution(929879968711143295)
XLA Ops:
  0.0 416.2 %shard_map.37 = f32[8,256,256]{2,1,0:T(8,128)} custom-call(f32[8,256,256]{2,1,0:T(8,128)} %field_in.1, bf16[256,768]{1,0:T(8,128)(2,1)} %constant.4.clone.left, bf16[768,256]{1,0:T(8,128)(2,1)} %constant.5.clone.right), custom_call_target="tpu_custom_call" | custom-call | tf_op jit(solution)/shard_map/pallas_call | solution.py:422
  416.2 3.0 copy.5
